TPU v7x, 256 devices: a whole 4x4x8 slice. The times are simulated.
256 devices in a mesh: py: 8 (over z), px: 16 (over y, x), shift: 2 (over core).
Axes of the slice: x: 4, y: 4, z: 8, core: 2. Of those that a mesh axis runs over, the one named last changes fastest.
Arguments:
- right_side: float32 [1024, 1024, 256], P(('shift', 'py'), 'px'), parts along dimension 0, may hold values from -6 to 6
- first_guess: float32 [1024, 1024, 256], P(('shift', 'py'), 'px'), parts along dimension 0, may hold values from -6 to 6
- mass_term: float32 [1024, 1024, 256], P(('shift', 'py'), 'px'), parts along dimension 0, may hold values from 0.1 to 0.9
Outputs:
- corrected: float32 [1024, 1024, 256], P(('shift', 'py'), 'px'), parts along dimension 0
- remaining: float32 [1024, 1024, 256], P(('shift', 'py'), 'px'), parts along dimension 0
There are 2 independent parts, one for each index of `shift`. A program takes and returns all parts, laid end to end along the dimension named above; each array names one. Nothing has to cross between parts.
All inputs are finite; a program needn't handle non-finite values.
Results may differ from a plain program's by a relative error of at most 0.000031.
Values sent between devices are 32-bit elements.
A program may use at most 128 MiB of HBM per device.

v0:
```python
import jax
import jax.numpy as jnp
from jax import lax
from jax.experimental import pallas as pl
from jax.experimental.pallas import tpu as pltpu
from jax.sharding import PartitionSpec as P

RATIO = 4
H, L = 2, 128
B = 64
C = B // RATIO
Y0, X0, YS, XS = 4, 12, 72, 88
D = 9
CX0, CXS = 11, 40
EX0, EXS = 8, 104
ANY = pl.BlockSpec(memory_space=pl.ANY)
VMEM = pl.BlockSpec(memory_space=pltpu.VMEM)
FINE = (H, YS, XS, L)
COARSE = (H, C + 2 * D, CXS, L)
SPREAD = (H, C + 4, EXS, L)


def tiles(first, last):
    starts = list(range(first, last - 7, 8))
    if starts[-1] + 8 < last:
        starts.append(last - 8)
    return starts


def group_of(count, best=(4, 6, 5, 3, 2)):
    return next(g for g in (*best, 1) if count % g == 0)


def rows_loop(first, last, body, best=(4, 6, 5, 3, 2)):
    g = group_of(last - first, best)

    def step(i, carry):
        body(first + i * g, g)
        return carry

    lax.fori_loop(0, (last - first) // g, step, 0)


def near_sum(src, h, y, x, g):
    column = [src[h, y + k, pl.ds(x, 8), :] for k in range(-1, g + 1)]
    sums = []
    for k in range(g):
        left = src[h, y + k, pl.ds(x - 1, 8), :]
        right = src[h, y + k, pl.ds(x + 1, 8), :]
        sums.append((column[k] + column[k + 2]) + (left + right))
    return column[1:-1], sums


def sweep(dst, src, load, weight, ys, xs, y0=Y0, x0=X0):
    def body(y, g):
        for h in range(H):
            for x in tiles(*xs):
                centre, near = near_sum(src, h, y + y0, x + x0, g)
                for k in range(g):
                    at = (h, y + y0 + k, pl.ds(x + x0, 8), slice(None))
                    dst[at] = 0.2 * centre[k] + weight[at] * (load[at] + near[k])

    rows_loop(*ys, body)


def weigh(dst, mass, ys, xs, y0=Y0, x0=X0, best=(4, 6, 5, 3, 2)):
    def body(y, g):
        for h in range(H):
            for x in tiles(*xs):
                for k in range(g):
                    at = (h, y + y0 + k, pl.ds(x + x0, 8), slice(None))
                    dst[at] = 0.8 / (4.0 + mass[at])

    rows_loop(*ys, body, best)


def block_sums(dst, sums):
    def body(y, g):
        for k in range(g):
            for h in range(H):
                for t in range(C // 8):
                    parts = [sums[y + k, h, pl.ds(32 * t + j, 8, stride=4), :] for j in range(4)]
                    dst[h, y + k + D, pl.ds(CX0 + 8 * t, 8), :] = 0.25 * (
                        (parts[0] + parts[1]) + (parts[2] + parts[3])
                    )

    rows_loop(0, C, body)


class Halo:
    def __init__(self, buffer, size, y0, x0, depths, corners, around, send, recv, base):
        self.copies = []
        lo, hi = depths

        def add(dy, dx, ys, xs):
            src = buffer.at[:, pl.ds(y0 + ys[0], ys[1]), pl.ds(x0 + xs[0], xs[1]), :]
            dst = buffer.at[
                :, pl.ds(y0 + ys[0] - dy * size, ys[1]), pl.ds(x0 + xs[0] - dx * size, xs[1]), :
            ]
            n = base + len(self.copies)
            self.copies.append(
                pltpu.make_async_remote_copy(
                    src_ref=src,
                    dst_ref=dst,
                    send_sem=send.at[n],
                    recv_sem=recv.at[n],
                    device_id=around(dy, dx),
                    device_id_type=pl.DeviceIdType.MESH,
                )
            )

        def span(d, low, high):
            return (size - high, high - low) if d > 0 else (low, high - low)

        for (ya, yb), (xa, xb) in corners:
            for dy in (1, -1):
                for dx in (1, -1):
                    add(dy, dx, span(dy, ya, yb), span(dx, xa, xb))
        for d in (1, -1):
            add(0, d, (0, size), span(d, lo, hi))
        for d in (1, -1):
            add(d, 0, span(d, lo, hi), (0, size))

    def start(self):
        for c in self.copies:
            c.start()

    def arrive(self):
        for c in self.copies:
            c.wait_recv()

    def sent(self):
        for c in self.copies:
            c.wait_send()


def first_kernel(
    right, guess, mass, v3, r, w, e, m, u, v1, v2, cl, cm, cw, ca, cb, sums, local, send, recv
):
    npy, npx = lax.axis_size("py"), lax.axis_size("px")
    py, px = lax.axis_index("py"), lax.axis_index("px")

    def around(dy, dx):
        return {"py": lax.rem(py + dy + npy, npy), "px": lax.rem(px + dx + npx, npx)}

    loads = []
    for i, (src, dst) in enumerate(((guess, u), (right, r), (mass, m))):
        loads.append(
            [
                pltpu.make_async_copy(
                    src.at[:, :, pl.ds(h * L, L)],
                    dst.at[h, pl.ds(Y0, B), pl.ds(X0, B), :],
                    local.at[i, h],
                )
                for h in range(H)
            ]
        )
        for c in loads[-1]:
            c.start()

    barrier = pltpu.get_barrier_semaphore()
    ring = [(dy, dx) for dy in (-1, 0, 1) for dx in (-1, 0, 1) if (dy, dx) != (0, 0)]
    for dy, dx in ring:
        pl.semaphore_signal(
            barrier, inc=1, device_id=around(dy, dx), device_id_type=pl.DeviceIdType.MESH
        )
    pl.semaphore_wait(barrier, len(ring))

    halos = []

    def halo(buffer, size, y0, x0, depths, corners):
        base = sum(len(one.copies) for one in halos)
        halos.append(Halo(buffer, size, y0, x0, depths, corners, around, send, recv, base))
        return halos[-1]

    square = lambda n: [((0, n), (0, n))]
    fine = lambda buffer, depths, corners: halo(buffer, B, Y0, X0, depths, corners)
    wedge = [((0, 4), (0, 8)), ((4, 8), (0, 4))]

    for c in loads[0]:
        c.wait()
    u_halo = fine(u, (0, 3), square(2))
    u_halo.start()
    for c in loads[1]:
        c.wait()
    r_halo = fine(r, (0, 2), square(2))
    r_halo.start()
    for c in loads[2]:
        c.wait()
    m_halo = fine(m, (0, 2), square(2))
    m_halo.start()

    def mass_rows(y, g):
        for k in range(g):
            for h in range(H):
                for x in tiles(0, B):
                    parts = [m[h, Y0 + 4 * (y + k) + j, pl.ds(X0 + x, 8), :] for j in range(4)]
                    sums[y + k, h, pl.ds(x, 8), :] = (parts[0] + parts[1]) + (parts[2] + parts[3])

    rows_loop(0, C, mass_rows, (2,))
    block_sums(cm, sums)
    cm_halo = halo(cm, C, D, CX0, (0, D), wedge)
    cm_halo.start()
    r_more = fine(r, (2, 3), [])
    r_more.start()
    m_more = fine(m, (2, 3), [])
    m_more.start()

    weigh(w, m, (0, B), (0, B))

    u_halo.arrive()
    r_halo.arrive()
    m_halo.arrive()
    weigh(w, m, (-2, 0), (-2, B + 2))
    weigh(w, m, (B, B + 2), (-2, B + 2))
    weigh(w, m, (0, B), (-2, 6))
    weigh(w, m, (0, B), (B - 6, B + 2))
    sweep(v1, u, r, w, (-2, B + 2), (-2, B + 2))
    sweep(v2, v1, r, w, (0, B), (-1, B + 1))
    sweep(v2, v1, r, w, (-1, 0), (0, B))
    sweep(v2, v1, r, w, (B, B + 1), (0, B))

    def defect_rows(y, g):
        for h in range(H):
            for x in tiles(0, B):
                centre, near = near_sum(v2, h, Y0 + 4 * y, X0 + x, 4)
                parts = []
                for k in range(4):
                    at = (h, Y0 + 4 * y + k, pl.ds(X0 + x, 8), slice(None))
                    parts.append(r[at] + near[k] - (4.0 + m[at]) * centre[k])
                sums[y, h, pl.ds(x, 8), :] = (parts[0] + parts[1]) + (parts[2] + parts[3])

    rows_loop(0, C, defect_rows, (1,))
    block_sums(cl, sums)
    cl_halo = halo(cl, C, D, CX0, (0, D), wedge)
    cl_halo.start()
    v2_halo = fine(v2, (1, 4), square(3))
    v2_halo.start()

    cm_halo.arrive()
    weigh(cw, cm, (-D, C + D), (-D, C + D), D, CX0)
    cl_halo.arrive()

    def first_coarse(y, g):
        for h in range(H):
            for x in tiles(-D, C + D):
                for k in range(g):
                    at = (h, y + D + k, pl.ds(x + CX0, 8), slice(None))
                    ca[at] = cw[at] * cl[at]

    rows_loop(-D, C + D, first_coarse, (2,))
    here, there = ca, cb
    for n in range(D - 1, 0, -1):
        sweep(there, here, cl, cw, (-n, C + n), (-n, C + n), D, CX0)
        here, there = there, here

    def spread(y, g):
        for k in range(g):
            for h in range(H):
                for t in range(3):
                    value = here[h, y + k + D, pl.ds(CX0 - 1 + 8 * t, 8), :]
                    for j in range(4):
                        e[h, y + k + 2, pl.ds(EX0 - 4 + 32 * t + j, 8, stride=4), :] = value

    rows_loop(-1, C + 1, spread, (2,))

    r_more.arrive()
    m_more.arrive()
    v2_halo.arrive()
    weigh(w, m, (-3, -2), (-3, B + 3), best=(1,))
    weigh(w, m, (B + 2, B + 3), (-3, B + 3), best=(1,))
    weigh(w, m, (-2, B + 2), (-3, 5))
    weigh(w, m, (-2, B + 2), (B - 5, B + 3))
    sweep(v3, v2, r, w, (-3, B + 3), (-3, B + 3))
    for one in halos:
        one.sent()


def second_kernel(v3, r, w, e, mass, corrected, remaining, a, b, m, sem, local):
    loads = [
        pltpu.make_async_copy(mass.at[:, :, pl.ds(h * L, L)], m.at[h], local.at[h])
        for h in range(H)
    ]
    for c in loads:
        c.start()

    def correct(y, g):
        for h in range(H):
            for x in tiles(-4, B + 4):
                at = lambda n, s=0: e[h, y + 2 + n, pl.ds(EX0 + x + s, 8), :]
                here, up, down = at(0), at(-1), at(1)
                sides = at(0, -1) + at(0, 1)
                small = 0.2 * here
                near = [sides + (up + here)] + [sides + (here + here)] * 2 + [sides + (here + down)]
                for k in range(4):
                    cell = (h, Y0 + 4 * y + k, pl.ds(X0 + x, 8), slice(None))
                    a[cell] = v3[cell] + (small + w[cell] * near[k])

    rows_loop(-1, C + 1, correct, (1,))
    sweep(b, a, r, w, (-2, B + 2), (-2, B + 2))
    sweep(a, b, r, w, (-1, B + 1), (-1, B + 1))

    copies = []

    def put(src, dst, i, first, count):
        for h in range(H):
            c = pltpu.make_async_copy(
                src.at[h, pl.ds(Y0 + first, count), pl.ds(X0, B), :],
                dst.at[pl.ds(first, count), :, pl.ds(h * L, L)],
                sem.at[i, h],
            )
            c.start()
            copies.append(c)

    put(a, corrected, 0, 0, B)

    def rest(y, g):
        for h in range(H):
            for x in tiles(0, B):
                centre, near = near_sum(a, h, Y0 + y, X0 + x, g)
                for k in range(g):
                    at = (h, Y0 + y + k, pl.ds(X0 + x, 8), slice(None))
                    heavy = 4.0 + m[h, y + k, pl.ds(x, 8), :]
                    b[at] = r[at] + near[k] - heavy * centre[k]

    for c in loads:
        c.wait()
    for q in range(4):
        rows_loop(16 * q, 16 * q + 16, rest)
        put(b, remaining, 1 + q, 16 * q, 16)
    for c in copies:
        c.wait()


def shards(right_side, first_guess, mass_term):
    f32 = jnp.float32
    copies = 4 * 8 + 2 * 12 + 2 * 4
    held = pl.pallas_call(
        first_kernel,
        out_shape=(*[pltpu.VMEM(FINE, f32)] * 3, pltpu.VMEM(SPREAD, f32)),
        in_specs=[ANY] * 3,
        out_specs=(VMEM,) * 4,
        scratch_shapes=[
            *[pltpu.VMEM(FINE, f32)] * 4,
            *[pltpu.VMEM(COARSE, f32)] * 5,
            pltpu.VMEM((C, H, B, L), f32),
            pltpu.SemaphoreType.DMA((3, H)),
            pltpu.SemaphoreType.DMA((copies,)),
            pltpu.SemaphoreType.DMA((copies,)),
        ],
        compiler_params=pltpu.CompilerParams(
            collective_id=0, has_side_effects=True, vmem_limit_bytes=40 << 20
        ),
        name="first",
    )(right_side, first_guess, mass_term)
    held = [pltpu.with_memory_space_constraint(one, pltpu.VMEM) for one in held]
    mass_term = pltpu.with_memory_space_constraint(mass_term, pltpu.HBM)
    block = jax.ShapeDtypeStruct(right_side.shape, f32)
    return pl.pallas_call(
        second_kernel,
        out_shape=(block, block),
        in_specs=[VMEM] * 4 + [ANY],
        out_specs=(ANY, ANY),
        scratch_shapes=[
            *[pltpu.VMEM(FINE, f32)] * 2,
            pltpu.VMEM((H, B, B, L), f32),
            pltpu.SemaphoreType.DMA((5, H)),
            pltpu.SemaphoreType.DMA((H,)),
        ],
        compiler_params=pltpu.CompilerParams(vmem_limit_bytes=40 << 20),
        name="second",
    )(*held, mass_term)


def solution(mesh):
    spec = P(("shift", "py"), "px", None)
    return jax.shard_map(
        shards, mesh=mesh, in_specs=(spec,) * 3, out_specs=(spec,) * 2, check_vma=False
    )
```

profile of v0, /device:TPU:1, one launch (start us, length us, event | category | flops | bytes accessed | tf_op | source)
XLA Modules:
  0.0 50.1 jit_solution(17126012703260157324)
XLA Ops:
  0.6 42.3 %first.1 = (f32[2,72,88,128]{3,2,1,0:T(8,128)S(1)}, f32[2,72,88,128]{3,2,1,0:T(8,128)S(1)}, f32[2,72,88,128]{3,2,1,0:T(8,128)S(1)}, f32[2,20,104,128]{3,2,1,0:T(8,128)S(1)}) custom-call(f32[64,64,256]{2,1,0:T(8,128)} %right.1, f32[64,64,256]{2,1,0:T(8,128)} %guess.1, f32[64,64,256]{2,1,0:T(8,128)} %mass.3), custom_call_target="tpu_custom_call" | custom-call | tf_op jit(solution)/shard_map/first/pallas_call | solution.py:338
  43.0 7.1 %second.1 = (f32[64,64,256]{2,1,0:T(8,128)}, f32[64,64,256]{2,1,0:T(8,128)}) custom-call(f32[2,72,88,128]{3,2,1,0:T(8,128)S(1)} %get-tuple-element.6.v3, f32[2,72,88,128]{3,2,1,0:T(8,128)S(1)} %get-tuple-element.7.r, f32[2,72,88,128]{3,2,1,0:T(8,128)S(1)} %get-tuple-element.8.w, f32[2,20,104,128]{3,2,1,0:T(8,128)S(1)} %get-tuple-element.9.e, f32[64,64,256]{2,1,0:T(8,128)} %mass.3), custom_call_target="tpu_custom_call" | custom-call | tf_op jit(solution)/shard_map/second/pallas_call | solution.py:359
where the time goes:
time: 50.7 us; the launch traced here: 50.1 us
  Pallas kernels  49.4 us (97%)
  between operations  0.64 us (1%)
    pallas_call x1, Pallas kernels, shards(): pl.pallas_call(first_kernel, out_shape=(*[pltpu.VMEM(FINE, f32)] * 3, plt...  42.3 us
    pallas_call x1, Pallas kernels, shards(): pl.pallas_call(second_kernel, out_shape=(block, block), in_specs=[VMEM] *...  7.13 us

commit v1 on v0

v1 whole, which is shorter than its diff:
```python
import jax
import jax.numpy as jnp
from jax import lax
from jax.experimental import pallas as pl
from jax.experimental.pallas import tpu as pltpu
from jax.sharding import PartitionSpec as P

RATIO = 4
H, L = 2, 128
B = 64
C = B // RATIO
Y0, X0, YS, XS = 4, 12, 72, 88
D = 9
CX0, CXS = 11, 40
EX0, EXS = 8, 104
FIRST_CUTS, LAST_CUTS = (23, 47, B + 1), (24, 48, 60, B)
ANY = pl.BlockSpec(memory_space=pl.ANY)
VMEM = pl.BlockSpec(memory_space=pltpu.VMEM)
FINE = (H, YS, XS, L)
COARSE = (H, C + 2 * D, CXS, L)
SPREAD = (H, C + 4, EXS, L)


def tiles(first, last):
    starts = list(range(first, last - 7, 8))
    if starts[-1] + 8 < last:
        starts.append(last - 8)
    return starts


def rows_loop(first, last, body, g=4):
    whole = (last - first) // g

    def step(i, carry):
        body(first + i * g, g)
        return carry

    if whole > 1:
        lax.fori_loop(0, whole, step, 0)
    elif whole:
        body(first, g)
    if (last - first) % g:
        body(first + whole * g, (last - first) % g)


def near_sum(src, h, y, x, g):
    column = [src[h, y + k, pl.ds(x, 8), :] for k in range(-1, g + 1)]
    sums = []
    for k in range(g):
        left = src[h, y + k, pl.ds(x - 1, 8), :]
        right = src[h, y + k, pl.ds(x + 1, 8), :]
        sums.append((column[k] + column[k + 2]) + (left + right))
    return column[1:-1], sums


def sweep(dst, src, load, weight, ys, xs, y0=Y0, x0=X0):
    def body(y, g):
        for h in range(H):
            for x in tiles(*xs):
                centre, near = near_sum(src, h, y + y0, x + x0, g)
                for k in range(g):
                    at = (h, y + y0 + k, pl.ds(x + x0, 8), slice(None))
                    dst[at] = 0.2 * centre[k] + weight[at] * (load[at] + near[k])

    rows_loop(*ys, body)


def weigh(dst, mass, ys, xs, y0=Y0, x0=X0, g=4):
    def body(y, g):
        for h in range(H):
            for x in tiles(*xs):
                for k in range(g):
                    at = (h, y + y0 + k, pl.ds(x + x0, 8), slice(None))
                    dst[at] = 0.8 / (4.0 + mass[at])

    rows_loop(*ys, body, g)


def block_sums(dst, sums, ys):
    def body(y, g):
        for k in range(g):
            for h in range(H):
                for t in range(C // 8):
                    parts = [sums[y + k, h, pl.ds(32 * t + j, 8, stride=4), :] for j in range(4)]
                    dst[h, y + k + D, pl.ds(CX0 + 8 * t, 8), :] = 0.25 * (
                        (parts[0] + parts[1]) + (parts[2] + parts[3])
                    )

    rows_loop(*ys, body)


class Halo:
    def __init__(self, around, send, recv, halos):
        self.around, self.send, self.recv = around, send, recv
        self.base = sum(len(one.copies) for one in halos)
        self.copies = []
        halos.append(self)

    def add(self, buffer, size, y0, x0, dy, dx, ys, xs):
        n = self.base + len(self.copies)
        self.copies.append(
            pltpu.make_async_remote_copy(
                src_ref=buffer.at[:, pl.ds(y0 + ys[0], ys[1]), pl.ds(x0 + xs[0], xs[1]), :],
                dst_ref=buffer.at[
                    :, pl.ds(y0 + ys[0] - dy * size, ys[1]), pl.ds(x0 + xs[0] - dx * size, xs[1]), :
                ],
                send_sem=self.send.at[n],
                recv_sem=self.recv.at[n],
                device_id=self.around(dy, dx),
                device_id_type=pl.DeviceIdType.MESH,
            )
        )

    def edges(self, buffer, size, y0, x0, depths, along):
        low, high = depths
        along = (along[0], along[1] - along[0])
        for d in (1, -1):
            across = (size - high if d > 0 else low, high - low)
            self.add(buffer, size, y0, x0, 0, d, along, across)
            self.add(buffer, size, y0, x0, d, 0, across, along)

    def corners(self, buffer, size, y0, x0, rectangles):
        for (ya, yb), (xa, xb) in rectangles:
            for dy in (1, -1):
                for dx in (1, -1):
                    ys = (size - yb if dy > 0 else ya, yb - ya)
                    xs = (size - xb if dx > 0 else xa, xb - xa)
                    self.add(buffer, size, y0, x0, dy, dx, ys, xs)

    def start(self):
        for c in self.copies:
            c.start()

    def arrive(self):
        for c in self.copies:
            c.wait_recv()

    def sent(self):
        for c in self.copies:
            c.wait_send()


def first_kernel(
    right, guess, mass, v3, r, w, e, m, u, v1, v2, cl, cm, cw, ca, cb, sums, local, send, recv
):
    npy, npx = lax.axis_size("py"), lax.axis_size("px")
    py, px = lax.axis_index("py"), lax.axis_index("px")

    def around(dy, dx):
        return {"py": lax.rem(py + dy + npy, npy), "px": lax.rem(px + dx + npx, npx)}

    pieces = [((0, 4), (0, B)), ((B - 4, B), (0, B)), ((4, B - 4), (0, 8)), ((4, B - 4), (B - 8, B))]
    parts = [pieces, [((4, B - 4), (8, B - 8))]]
    whole = [[((0, B), (0, B))], []]
    loads = {}
    for part in range(2):
        for i, (src, dst) in enumerate(((guess, u), (right, r), (mass, m))):
            loads[i, part] = [
                pltpu.make_async_copy(
                    src.at[pl.ds(ya, yb - ya), pl.ds(xa, xb - xa), pl.ds(h * L, L)],
                    dst.at[h, pl.ds(Y0 + ya, yb - ya), pl.ds(X0 + xa, xb - xa), :],
                    local.at[i, 4 * part + n, h],
                )
                for n, ((ya, yb), (xa, xb)) in enumerate(whole[part])
                for h in range(H)
            ]
    for key in ((0, 0), (1, 0), (2, 0), (0, 1)):
        for c in loads[key]:
            c.start()

    def loaded(i, part):
        for c in loads[i, part]:
            c.wait()

    barrier = pltpu.get_barrier_semaphore()
    ring = [(dy, dx) for dy in (-1, 0, 1) for dx in (-1, 0, 1) if (dy, dx) != (0, 0)]
    for dy, dx in ring:
        pl.semaphore_signal(
            barrier, inc=1, device_id=around(dy, dx), device_id_type=pl.DeviceIdType.MESH
        )
    pl.semaphore_wait(barrier, len(ring))

    halos = []

    def halo(buffer, size, y0, x0, depths, rectangles):
        one = Halo(around, send, recv, halos)
        one.corners(buffer, size, y0, x0, rectangles)
        one.edges(buffer, size, y0, x0, depths, (0, size))
        return one

    square = lambda n: [((0, n), (0, n))]
    fine = lambda buffer, depths, rectangles: halo(buffer, B, Y0, X0, depths, rectangles)
    wedge = [((n, min(n + 2, D)), (0, D - n)) for n in range(0, D, 2)]

    loaded(0, 0)
    u_halo = fine(u, (0, 3), square(2))
    u_halo.start()
    loaded(1, 0)
    r_halo = fine(r, (0, 2), square(2))
    r_halo.start()
    loaded(2, 0)
    m_halo = fine(m, (0, 2), square(2))
    m_halo.start()

    def mass_rows(y, g):
        for k in range(g):
            for h in range(H):
                for x in tiles(0, B):
                    parts = [m[h, Y0 + 4 * (y + k) + j, pl.ds(X0 + x, 8), :] for j in range(4)]
                    sums[y + k, h, pl.ds(x, 8), :] = (parts[0] + parts[1]) + (parts[2] + parts[3])

    loaded(2, 1)
    rows_loop(0, C, mass_rows, 1)
    block_sums(cm, sums, (0, C))
    cm_halo = halo(cm, C, D, CX0, (0, D), wedge)
    cm_halo.start()
    m_more = fine(m, (2, 3), [])
    m_more.start()

    def defect(ys, xs):
        def body(y, g):
            for k in range(g):
                for h in range(H):
                    for x in tiles(*xs):
                        centre, near = near_sum(v2, h, Y0 + 4 * (y + k), X0 + x, 4)
                        parts = []
                        for j in range(4):
                            at = (h, Y0 + 4 * (y + k) + j, pl.ds(X0 + x, 8), slice(None))
                            parts.append(r[at] + near[j] - (4.0 + m[at]) * centre[j])
                        sums[y + k, h, pl.ds(x, 8), :] = (parts[0] + parts[1]) + (
                            parts[2] + parts[3]
                        )

        rows_loop(*ys, body, 1)

    weigh(w, m, (0, B), (0, B))
    loaded(0, 1)
    loaded(1, 1)
    sweep(v1, u, r, w, (2, B - 2), (2, B - 2))
    sweep(v2, v1, r, w, (3, B - 3), (3, B - 3))
    defect((1, C - 1), (4, B - 4))

    u_halo.arrive()
    r_halo.arrive()
    m_halo.arrive()
    for ys in ((-2, 0), (B, B + 2)):
        weigh(w, m, ys, (-2, B + 2))
    for xs in ((-2, 6), (B - 6, B + 2)):
        weigh(w, m, (0, B), xs)
    for ys in ((-2, 2), (B - 2, B + 2)):
        sweep(v1, u, r, w, ys, (-2, B + 2))
    for xs in ((-2, 6), (B - 6, B + 2)):
        sweep(v1, u, r, w, (2, B - 2), xs)
    for ys in ((-1, 3), (B - 3, B + 1)):
        sweep(v2, v1, r, w, ys, (0, B))
    for xs in ((-1, 7), (B - 7, B + 1)):
        sweep(v2, v1, r, w, (0, B), xs)
    for ys in ((0, 1), (C - 1, C)):
        defect(ys, (0, B))
    for xs in ((0, 8), (B - 8, B)):
        defect((1, C - 1), xs)
    block_sums(cl, sums, (0, C))
    cl_halo = halo(cl, C, D, CX0, (0, D), wedge)
    cl_halo.start()

    sweep(v3, v2, r, w, (0, B), (0, B))
    v3_halo = fine(v3, (0, 3), square(2))
    v3_halo.start()
    cm_halo.arrive()
    weigh(cw, cm, (-D, C + D), (-D, C + D), D, CX0)
    cl_halo.arrive()

    def first_coarse(y, g):
        for h in range(H):
            for x in tiles(-D, C + D):
                for k in range(g):
                    at = (h, y + D + k, pl.ds(x + CX0, 8), slice(None))
                    ca[at] = cw[at] * cl[at]

    rows_loop(-D, C + D, first_coarse, 2)
    here, there = ca, cb
    for n in range(D - 1, 0, -1):
        sweep(there, here, cl, cw, (-n, C + n), (-n, C + n), D, CX0)
        here, there = there, here

    def spread(y, g):
        for k in range(g):
            for h in range(H):
                for t in range(3):
                    value = here[h, y + k + D, pl.ds(CX0 - 1 + 8 * t, 8), :]
                    for j in range(4):
                        e[h, y + k + 2, pl.ds(EX0 - 4 + 32 * t + j, 8, stride=4), :] = value

    rows_loop(-1, C + 1, spread, 1)

    m_more.arrive()
    for ys in ((-3, -2), (B + 2, B + 3)):
        weigh(w, m, ys, (0, B))
    for xs in ((-3, 5), (B - 5, B + 3)):
        weigh(w, m, (0, B), xs)
    v3_halo.arrive()
    for one in halos:
        one.sent()


def second_kernel(v3, r, w, e, mass, corrected, remaining, a, b, m, sem, local):
    loads = [
        pltpu.make_async_copy(mass.at[:, :, pl.ds(h * L, L)], m.at[h], local.at[h])
        for h in range(H)
    ]
    for c in loads:
        c.start()

    def correct(y, g):
        for h in range(H):
            for x in tiles(-4, B + 4):
                at = lambda n, s=0: e[h, y + 2 + n, pl.ds(EX0 + x + s, 8), :]
                here, up, down = at(0), at(-1), at(1)
                sides = at(0, -1) + at(0, 1)
                small = 0.2 * here
                near = [sides + (up + here)] + [sides + (here + here)] * 2 + [sides + (here + down)]
                for k in range(4):
                    cell = (h, Y0 + 4 * y + k, pl.ds(X0 + x, 8), slice(None))
                    a[cell] = v3[cell] + (small + w[cell] * near[k])

    rows_loop(-1, C + 1, correct, 1)
    sweep(b, a, r, w, (-2, B + 2), (-2, B + 2))
    copies = []

    def put(src, dst, i, first, count):
        for h in range(H):
            c = pltpu.make_async_copy(
                src.at[h, pl.ds(Y0 + first, count), pl.ds(X0, B), :],
                dst.at[pl.ds(first, count), :, pl.ds(h * L, L)],
                sem.at[i, h],
            )
            c.start()
            copies.append(c)

    last = -1
    for i, upto in enumerate(FIRST_CUTS):
        sweep(a, b, r, w, (last, upto), (-1, B + 1))
        put(a, corrected, i, max(last, 0), min(upto, B) - max(last, 0))
        last = upto

    def rest(y, g):
        for h in range(H):
            for x in tiles(0, B):
                centre, near = near_sum(a, h, Y0 + y, X0 + x, g)
                for k in range(g):
                    at = (h, Y0 + y + k, pl.ds(X0 + x, 8), slice(None))
                    heavy = 4.0 + m[h, y + k, pl.ds(x, 8), :]
                    b[at] = r[at] + near[k] - heavy * centre[k]

    for c in loads:
        c.wait()
    last = 0
    for i, upto in enumerate(LAST_CUTS):
        rows_loop(last, upto, rest)
        put(b, remaining, len(FIRST_CUTS) + i, last, upto - last)
        last = upto
    for c in copies:
        c.wait()


def shards(right_side, first_guess, mass_term):
    f32 = jnp.float32
    copies = 4 * 8 + 2 * 24 + 4
    held = pl.pallas_call(
        first_kernel,
        out_shape=(*[pltpu.VMEM(FINE, f32)] * 3, pltpu.VMEM(SPREAD, f32)),
        in_specs=[ANY] * 3,
        out_specs=(VMEM,) * 4,
        scratch_shapes=[
            *[pltpu.VMEM(FINE, f32)] * 4,
            *[pltpu.VMEM(COARSE, f32)] * 5,
            pltpu.VMEM((C, H, B, L), f32),
            pltpu.SemaphoreType.DMA((3, 5, H)),
            pltpu.SemaphoreType.DMA((copies,)),
            pltpu.SemaphoreType.DMA((copies,)),
        ],
        compiler_params=pltpu.CompilerParams(
            collective_id=0, has_side_effects=True, vmem_limit_bytes=40 << 20
        ),
        name="first",
    )(right_side, first_guess, mass_term)
    held = [pltpu.with_memory_space_constraint(one, pltpu.VMEM) for one in held]
    mass_term = pltpu.with_memory_space_constraint(mass_term, pltpu.HBM)
    block = jax.ShapeDtypeStruct(right_side.shape, f32)
    return pl.pallas_call(
        second_kernel,
        out_shape=(block, block),
        in_specs=[VMEM] * 4 + [ANY],
        out_specs=(ANY, ANY),
        scratch_shapes=[
            *[pltpu.VMEM(FINE, f32)] * 2,
            pltpu.VMEM((H, B, B, L), f32),
            pltpu.SemaphoreType.DMA((len(FIRST_CUTS) + len(LAST_CUTS), H)),
            pltpu.SemaphoreType.DMA((H,)),
        ],
        compiler_params=pltpu.CompilerParams(vmem_limit_bytes=40 << 20),
        name="second",
    )(*held, mass_term)


def solution(mesh):
    spec = P(("shift", "py"), "px", None)
    return jax.shard_map(
        shards, mesh=mesh, in_specs=(spec,) * 3, out_specs=(spec,) * 2, check_vma=False
    )
```

time: 50.7 us -> 47.2 us (0.931); the launches traced: 50.1 us -> 47.2 us
  Pallas kernels: 49.4 us -> 46.5 us
    pallas_call x1, Pallas kernels: 42.3 us -> 40.1 us  [shards(): pl.pallas_call(first_kernel, out_shape=(*[pltpu.VMEM(FINE, f32)] * 3, plt...]
    pallas_call x1, Pallas kernels: 7.13 us -> 6.4 us  [shards(): pl.pallas_call(second_kernel, out_shape=(block, block), in_specs=[VMEM] *...]
where the time goes in v1:
time: 47.2 us
  Pallas kernels  46.5 us (99%)
  between operations  0.64 us (1%)
    pallas_call x1, Pallas kernels, shards(): pl.pallas_call(first_kernel, out_shape=(*[pltpu.VMEM(FINE, f32)] * 3, plt...  40.1 us
    pallas_call x1, Pallas kernels, shards(): pl.pallas_call(second_kernel, out_shape=(block, block), in_specs=[VMEM] *...  6.4 us

profile of v1, /device:TPU:1, one launch (start us, length us, event | category | flops | bytes accessed | tf_op | source)
XLA Modules:
  0.0 47.2 jit_solution(8828809256530646500)
XLA Ops:
  0.6 40.1 %first.1 = (f32[2,72,88,128]{3,2,1,0:T(8,128)S(1)}, f32[2,72,88,128]{3,2,1,0:T(8,128)S(1)}, f32[2,72,88,128]{3,2,1,0:T(8,128)S(1)}, f32[2,20,104,128]{3,2,1,0:T(8,128)S(1)}) custom-call(f32[64,64,256]{2,1,0:T(8,128)} %right.1, f32[64,64,256]{2,1,0:T(8,128)} %guess.1, f32[64,64,256]{2,1,0:T(8,128)} %mass.3), custom_call_target="tpu_custom_call" | custom-call | tf_op jit(solution)/shard_map/first/pallas_call | solution.py:369
  40.8 6.4 %second.1 = (f32[64,64,256]{2,1,0:T(8,128)}, f32[64,64,256]{2,1,0:T(8,128)}) custom-call(f32[2,72,88,128]{3,2,1,0:T(8,128)S(1)} %get-tuple-element.6.v3, f32[2,72,88,128]{3,2,1,0:T(8,128)S(1)} %get-tuple-element.7.r, f32[2,72,88,128]{3,2,1,0:T(8,128)S(1)} %get-tuple-element.8.w, f32[2,20,104,128]{3,2,1,0:T(8,128)S(1)} %get-tuple-element.9.e, f32[64,64,256]{2,1,0:T(8,128)} %mass.3), custom_call_target="tpu_custom_call" | custom-call | tf_op jit(solution)/shard_map/second/pallas_call | solution.py:390

commit v2 on v1

--- a/solution.py
+++ b/solution.py
@@ -126,6 +126,16 @@
                     ys = (size - yb if dy > 0 else ya, yb - ya)
                     xs = (size - xb if dx > 0 else xa, xb - xa)
                     self.add(buffer, size, y0, x0, dy, dx, ys, xs)
+
+    def relayed(self, buffer, size, y0, x0, rectangles):
+        for (ya, yb), (xa, xb) in rectangles:
+            for d in (1, -1):
+                near_y = (size - yb if d > 0 else ya, yb - ya)
+                near_x = (size - xb if d > 0 else xa, xb - xa)
+                far_y = (size + ya if d > 0 else -yb, yb - ya)
+                far_x = (-xb if d > 0 else size + xa, xb - xa)
+                self.add(buffer, size, y0, x0, d, 0, near_y, far_x)
+                self.add(buffer, size, y0, x0, 0, d, far_y, near_x)
 
     def start(self):
         for c in self.copies:
@@ -212,7 +222,7 @@
     loaded(2, 1)
     rows_loop(0, C, mass_rows, 1)
     block_sums(cm, sums, (0, C))
-    cm_halo = halo(cm, C, D, CX0, (0, D), wedge)
+    cm_halo = halo(cm, C, D, CX0, (0, D), [])
     cm_halo.start()
     m_more = fine(m, (2, 3), [])
     m_more.start()
@@ -263,11 +273,20 @@
     cl_halo = halo(cl, C, D, CX0, (0, D), wedge)
     cl_halo.start()
 
+    cm_halo.arrive()
+    cm_far = Halo(around, send, recv, halos)
+    cm_far.relayed(cm, C, D, CX0, wedge)
+    cm_far.start()
     sweep(v3, v2, r, w, (0, B), (0, B))
     v3_halo = fine(v3, (0, 3), square(2))
     v3_halo.start()
-    cm_halo.arrive()
-    weigh(cw, cm, (-D, C + D), (-D, C + D), D, CX0)
+    weigh(cw, cm, (0, C), (-D, C + D), D, CX0)
+    for ys in ((-D, 0), (C, C + D)):
+        weigh(cw, cm, ys, (0, C), D, CX0)
+    cm_far.arrive()
+    for ys in ((-D, 0), (C, C + D)):
+        for xs in ((-D, 0), (C, C + D)):
+            weigh(cw, cm, ys, xs, D, CX0)
     cl_halo.arrive()
 
     def first_coarse(y, g):

time: 47.2 us -> 47.7 us (1.011)
  Pallas kernels: 46.5 us -> 47 us
where the time goes in v2:
time: 47.7 us; the launch traced here: 47.6 us
  Pallas kernels  47 us (99%)
  between operations  0.64 us (1%)
    pallas_call x1, Pallas kernels, shards(): pl.pallas_call(first_kernel, out_shape=(*[pltpu.VMEM(FINE, f32)] * 3, plt...  40.6 us
    pallas_call x1, Pallas kernels, shards(): pl.pallas_call(second_kernel, out_shape=(block, block), in_specs=[VMEM] *...  6.4 us

profile of v2, /device:TPU:1, one launch (start us, length us, event | category | flops | bytes accessed | tf_op | source)
XLA Modules:
  0.0 47.6 jit_solution(3170418177641851595)
XLA Ops:
  0.6 40.6 %first.1 = (f32[2,72,88,128]{3,2,1,0:T(8,128)S(1)}, f32[2,72,88,128]{3,2,1,0:T(8,128)S(1)}, f32[2,72,88,128]{3,2,1,0:T(8,128)S(1)}, f32[2,20,104,128]{3,2,1,0:T(8,128)S(1)}) custom-call(f32[64,64,256]{2,1,0:T(8,128)} %right.1, f32[64,64,256]{2,1,0:T(8,128)} %guess.1, f32[64,64,256]{2,1,0:T(8,128)} %mass.3), custom_call_target="tpu_custom_call" | custom-call | tf_op jit(solution)/shard_map/first/pallas_call | solution.py:388
  41.2 6.4 %second.1 = (f32[64,64,256]{2,1,0:T(8,128)}, f32[64,64,256]{2,1,0:T(8,128)}) custom-call(f32[2,72,88,128]{3,2,1,0:T(8,128)S(1)} %get-tuple-element.6.v3, f32[2,72,88,128]{3,2,1,0:T(8,128)S(1)} %get-tuple-element.7.r, f32[2,72,88,128]{3,2,1,0:T(8,128)S(1)} %get-tuple-element.8.w, f32[2,20,104,128]{3,2,1,0:T(8,128)S(1)} %get-tuple-element.9.e, f32[64,64,256]{2,1,0:T(8,128)} %mass.3), custom_call_target="tpu_custom_call" | custom-call | tf_op jit(solution)/shard_map/second/pallas_call | solution.py:409
